TPU v7x, 32 devices: a whole 2x2x4 slice. The times are simulated.
32 devices in a mesh: members: 2 (over y), band: 4 (over z), head: 4 (over x, core).
Axes of the slice: x: 2, y: 2, z: 4, core: 2. Of those that a mesh axis runs over, the one named last changes fastest.
Arguments:
- grid_feats: bfloat16 [4096, 1024], P(('members', 'band')), parts along dimension 0, may hold values from -6 to 6
- mesh_feats: bfloat16 [4096, 1024], P(('members', 'band')), parts along dimension 0, may hold values from -6 to 6
- enc_in: bfloat16 [3, 1024, 1024], P(None, 'band', 'head'), may hold values from -0.19921875 to 0.19921875
- enc_out: bfloat16 [1024, 1024], P('head', 'band'), may hold values from -0.1875 to 0.1875
- proc_in: bfloat16 [3, 1024, 1024], P(None, 'band', 'head'), may hold values from -0.19921875 to 0.19921875
- proc_out: bfloat16 [1024, 1024], P('head', 'band'), may hold values from -0.1875 to 0.1875
- ff_up: bfloat16 [1024, 4096], P('band', 'head'), may hold values from -0.1875 to 0.1875
- ff_down: bfloat16 [4096, 1024], P('head', 'band'), may hold values from -0.09375 to 0.09375
- dec_in: bfloat16 [3, 1024, 1024], P(None, 'band', 'head'), may hold values from -0.19921875 to 0.19921875
- dec_out: bfloat16 [1024, 1024], P('head', 'band'), may hold values from -0.1875 to 0.1875
- enc_list: int32 [16, 8], replicated, may hold values from 0 to 15, as said below
- enc_count: int32 [16], replicated, may hold values from 1 to 8
- dec_list: int32 [16, 8], replicated, may hold values from 0 to 15, as said below
- dec_count: int32 [16], replicated, may hold values from 1 to 8
- window_ids: int32 [2048], replicated, may hold values from 0 to 1, never falling along the last dimension, each value on 1 to 1536 neighbouring positions
Outputs:
- grid_out: bfloat16 [4096, 1024], P(('members', 'band', 'head')), parts along dimension 0
There are 2 independent parts, one for each index of `members`. A program takes and returns all parts, laid end to end along the dimension named above; an argument that names none is the same for every part. Nothing has to cross between parts.
Inputs may be any that keep to these rules, and one draw needn't show every extreme that they name: `enc_list`: each row holds distinct block numbers. Every block listed for mesh block m lies in the band of 512 grid points with the same band number as m's band of 512 nodes, or in the band just before or just after it. Only the first enc_count[m] slots of row m of enc_list are used. `dec_list`: each row holds distinct block numbers. Every block listed for grid block g lies in the band of 512 mesh nodes with the same band number as g's band of 512 grid points, or in the band just before or just after it. Only the first dec_count[g] slots of row g of dec_list are used. `window_ids`: never falls along the nodes; each window holds at most 1536 consecutive nodes.
All inputs are finite; a program needn't handle non-finite values.
Results may differ from a plain program's by a relative error of at most 0.02.
Values may be sent and summed in bfloat16 or wider, within the bound.
No kernel may reach another device: no remote copies, remote signals or barrier semaphores. Data moves between devices by JAX's collectives and lax.ppermute only.
A program may use at most 64 MiB of HBM per device.

v0:
```python
import jax
import jax.numpy as jnp
from jax import lax
from jax.sharding import PartitionSpec as P

HD = 64
BLOCK = 128
WINDOW = 1536
EPSILON = 1e-05
NEGATIVE = -1e30


def padded(block, sides, width):
    for axis, dim in sides:
        count = lax.axis_size(axis)
        forward = [(i, i + 1) for i in range(count - 1)]
        backward = [(target, source) for source, target in forward]
        low = lax.ppermute(
            lax.slice_in_dim(block, block.shape[dim] - width, None, axis=dim), axis, forward
        )
        high = lax.ppermute(lax.slice_in_dim(block, 0, width, axis=dim), axis, backward)
        block = jnp.concatenate([low, block, high], axis=dim)
    return block


def shifted(block, axis, distance):
    devices = range(lax.axis_size(axis))
    route = [(i - distance, i) for i in devices if i - distance in devices]
    return lax.ppermute(block, axis, route)


def normed(source):
    values_f = source.astype(jnp.float32)
    centred = values_f - jnp.mean(values_f, axis=-1, keepdims=True)
    variance = jnp.mean(centred * centred, axis=-1, keepdims=True)
    return (centred * lax.rsqrt(variance + EPSILON)).astype(jnp.bfloat16)


def fold_three(sources, carry, piece):
    width = piece.shape[1]
    return tuple(
        (
            total
            + jnp.dot(
                lax.slice_in_dim(source, 0, width, axis=1),
                piece[which],
                preferred_element_type=jnp.float32,
            )
            for which, (total, source) in enumerate(zip(carry, sources))
        )
    )


def fold_rows(source, total, piece):
    return total + jnp.dot(
        lax.slice_in_dim(source, 0, piece.shape[0], axis=1),
        piece,
        preferred_element_type=jnp.float32,
    )


def columns_of(source, piece):
    return jnp.dot(source, piece, preferred_element_type=jnp.float32)


def head_scores(queries, key_rows, head_index, allowed):
    lower = head_index * HD
    scores = jnp.einsum(
        "qd,kd->qk",
        queries[:, lower : lower + HD],
        key_rows[:, lower : lower + HD],
        preferred_element_type=jnp.float32,
    ) * HD ** (-0.5)
    scores = jnp.where(allowed, scores, NEGATIVE)
    maxima = jnp.max(scores, axis=1, keepdims=True)
    expo = jnp.where(allowed, jnp.exp(scores - maxima), 0.0)
    return (expo, maxima, jnp.sum(expo, axis=1, keepdims=True))


def attend_rounded(queries, key_rows, value_rows, allowed):
    outputs = []
    for head_index in range(queries.shape[1] // HD):
        expo, maxima, totals = head_scores(queries, key_rows, head_index, allowed)
        weights = (expo / totals).astype(jnp.bfloat16)
        lower = head_index * HD
        outputs.append(
            jnp.dot(weights, value_rows[:, lower : lower + HD], preferred_element_type=jnp.float32)
        )
    return jnp.concatenate(outputs, axis=1).astype(jnp.bfloat16)


def partial_attend(queries, key_rows, value_rows, allowed):
    outputs, maxima_all, totals_all = ([], [], [])
    for head_index in range(queries.shape[1] // HD):
        expo, maxima, totals = head_scores(queries, key_rows, head_index, allowed)
        lower = head_index * HD
        outputs.append(
            jnp.dot(
                expo,
                value_rows[:, lower : lower + HD].astype(jnp.float32),
                precision=lax.Precision.HIGHEST,
            )
        )
        maxima_all.append(maxima)
        totals_all.append(totals)
    return (
        jnp.concatenate(outputs, axis=1),
        jnp.concatenate(maxima_all, axis=1),
        jnp.concatenate(totals_all, axis=1),
    )


def listed_attend(queries, key_pool, value_pool, lists, counts, base_block, rounded):
    width = queries.shape[1]
    rows = queries.shape[0]
    pool_blocks = key_pool.shape[0] // BLOCK
    key_blocks = key_pool.reshape(pool_blocks, BLOCK, width)
    value_blocks = value_pool.reshape(pool_blocks, BLOCK, width)
    slots = lists.shape[1]

    def one_block(index):
        listed = lists[index] - base_block
        inside = (
            (listed >= 0)
            & (listed < pool_blocks)
            & (jnp.arange(slots, dtype=jnp.int32) < counts[index])
        )
        safe = jnp.clip(listed, 0, pool_blocks - 1)
        block_keys = key_blocks[safe].reshape(slots * BLOCK, width)
        block_values = value_blocks[safe].reshape(slots * BLOCK, width)
        allowed = jnp.repeat(inside, BLOCK)[None, :]
        block_queries = lax.dynamic_slice_in_dim(queries, index * BLOCK, BLOCK, 0)
        if rounded:
            return attend_rounded(block_queries, block_keys, block_values, allowed)
        return partial_attend(block_queries, block_keys, block_values, allowed)

    result = lax.map(one_block, jnp.arange(rows // BLOCK, dtype=jnp.int32))
    return jax.tree.map(lambda stacked: stacked.reshape(rows, stacked.shape[-1]), result)


def normalize(outputs, totals):
    rows = outputs.shape[0]
    heads_here = totals.shape[1]
    shaped = outputs.reshape(rows, heads_here, HD) / totals[:, :, None]
    return shaped.reshape(rows, heads_here * HD).astype(jnp.bfloat16)


def per_device(
    grid_feats,
    mesh_feats,
    enc_in,
    enc_out,
    proc_in,
    proc_out,
    ff_up,
    ff_down,
    dec_in,
    dec_out,
    enc_list,
    enc_count,
    dec_list,
    dec_count,
    window_ids,
):
    band_index = lax.axis_index("band")
    grid_rows = grid_feats.shape[0]
    mesh_rows = mesh_feats.shape[0]
    width = enc_in.shape[2]
    grid_blocks = grid_rows // BLOCK
    mesh_blocks = mesh_rows // BLOCK
    grid_norm = normed(grid_feats)
    mesh_norm = normed(mesh_feats)
    grid_zeros = jnp.zeros((grid_rows, width), jnp.float32)
    mesh_zeros = jnp.zeros((mesh_rows, width), jnp.float32)
    enc_q, enc_k, enc_v = fold_three(
        (mesh_norm, grid_norm, grid_norm),
        (mesh_zeros, grid_zeros, grid_zeros),
        lax.all_gather(enc_in, "band", axis=1, tiled=True),
    )
    enc_q = enc_q.astype(jnp.bfloat16)
    enc_k = enc_k.astype(jnp.bfloat16)
    enc_v = enc_v.astype(jnp.bfloat16)
    my_lists = lax.dynamic_slice_in_dim(enc_list, band_index * mesh_blocks, mesh_blocks, 0)
    my_counts = lax.dynamic_slice_in_dim(enc_count, band_index * mesh_blocks, mesh_blocks, 0)
    pool = padded(jnp.stack([enc_k, enc_v]), (("band", 1),), grid_rows)
    outputs, maxima, totals = listed_attend(
        enc_q, pool[0], pool[1], my_lists, my_counts, (band_index - 1) * grid_blocks, False
    )
    enc_attn = normalize(outputs, totals)
    enc_terms = columns_of(enc_attn, lax.all_gather(enc_out, "band", axis=1, tiled=True))
    mesh_state = mesh_feats.astype(jnp.float32) + lax.psum(
        enc_terms.astype(jnp.bfloat16), "head"
    ).astype(jnp.float32)
    proc_norm = normed(mesh_state)
    proc_q, proc_k, proc_v = fold_three(
        (proc_norm, proc_norm, proc_norm),
        (mesh_zeros, mesh_zeros, mesh_zeros),
        lax.all_gather(proc_in, "band", axis=1, tiled=True),
    )
    proc_q = proc_q.astype(jnp.bfloat16)
    pairs = jnp.stack([proc_k.astype(jnp.bfloat16), proc_v.astype(jnp.bfloat16)])
    reach = (WINDOW + mesh_rows - 2) // mesh_rows
    slab_parts = {0: pairs}
    for distance in range(1, reach + 1):
        for direction in (1, -1):
            slab_parts[direction * distance] = shifted(pairs, "band", -direction * distance)
    slab = jnp.concatenate([slab_parts[offset] for offset in range(-reach, reach + 1)], axis=1)
    padded_ids = jnp.pad(window_ids, (reach * mesh_rows, reach * mesh_rows), constant_values=-1)
    slab_ids = lax.dynamic_slice_in_dim(
        padded_ids, band_index * mesh_rows, (2 * reach + 1) * mesh_rows, 0
    )
    slab_start = (band_index - reach) * mesh_rows
    span = 2 * WINDOW

    def window_block(index):
        first = band_index * mesh_rows + index * BLOCK
        first_id = window_ids[first]
        window_start = jnp.sum((window_ids < first_id).astype(jnp.int32))
        local = window_start - slab_start
        block_keys = lax.dynamic_slice_in_dim(slab[0], local, span, 0)
        block_values = lax.dynamic_slice_in_dim(slab[1], local, span, 0)
        key_ids = lax.dynamic_slice_in_dim(slab_ids, local, span, 0)
        query_ids = lax.dynamic_slice_in_dim(window_ids, first, BLOCK, 0)
        block_queries = lax.dynamic_slice_in_dim(proc_q, index * BLOCK, BLOCK, 0)
        return attend_rounded(
            block_queries, block_keys, block_values, query_ids[:, None] == key_ids[None, :]
        )

    proc_attn = lax.map(window_block, jnp.arange(mesh_blocks, dtype=jnp.int32)).reshape(
        mesh_rows, width
    )
    proc_terms = columns_of(proc_attn, lax.all_gather(proc_out, "band", axis=1, tiled=True))
    mesh_mid = mesh_state + lax.psum(proc_terms.astype(jnp.bfloat16), "head").astype(jnp.float32)
    ff_norm = normed(mesh_mid)
    hidden = fold_rows(
        ff_norm,
        jnp.zeros((mesh_rows, ff_up.shape[1]), jnp.float32),
        lax.all_gather(ff_up, "band", axis=0, tiled=True),
    )
    hidden = jax.nn.gelu(hidden, approximate=False).astype(jnp.bfloat16)
    ff_terms = columns_of(hidden, lax.all_gather(ff_down, "band", axis=1, tiled=True))
    mesh_final = mesh_mid + lax.psum(ff_terms.astype(jnp.bfloat16), "head").astype(jnp.float32)
    final_norm = normed(mesh_final)
    dec_q, dec_k, dec_v = fold_three(
        (grid_norm, final_norm, final_norm),
        (grid_zeros, mesh_zeros, mesh_zeros),
        lax.all_gather(dec_in, "band", axis=1, tiled=True),
    )
    dec_q = dec_q.astype(jnp.bfloat16)
    dec_pool = padded(
        jnp.stack([dec_k.astype(jnp.bfloat16), dec_v.astype(jnp.bfloat16)]),
        (("band", 1),),
        mesh_rows,
    )
    grid_lists = lax.dynamic_slice_in_dim(dec_list, band_index * grid_blocks, grid_blocks, 0)
    grid_counts = lax.dynamic_slice_in_dim(dec_count, band_index * grid_blocks, grid_blocks, 0)
    dec_attn = listed_attend(
        dec_q,
        dec_pool[0],
        dec_pool[1],
        grid_lists,
        grid_counts,
        (band_index - 1) * mesh_blocks,
        True,
    )
    full_out = lax.all_gather(dec_out, "band", axis=1, tiled=True)
    share = grid_rows // lax.axis_size("head")
    summed = lax.psum_scatter(
        jnp.dot(
            lax.slice_in_dim(dec_attn, 0, share * lax.axis_size("head"), axis=0),
            full_out,
            preferred_element_type=jnp.float32,
        ).astype(jnp.bfloat16),
        "head",
        scatter_dimension=0,
        tiled=True,
    ).astype(jnp.float32)
    residual = lax.dynamic_slice_in_dim(
        grid_feats, lax.axis_index("head") * share, share, 0
    ).astype(jnp.float32)
    return (residual + summed).astype(jnp.bfloat16)


def solution(mesh):
    return jax.shard_map(
        per_device,
        mesh=mesh,
        in_specs=(
            P(("members", "band"), None),
            P(("members", "band"), None),
            P(None, "band", "head"),
            P("head", "band"),
            P(None, "band", "head"),
            P("head", "band"),
            P("band", "head"),
            P("head", "band"),
            P(None, "band", "head"),
            P("head", "band"),
            P(),
            P(),
            P(),
            P(),
            P(),
        ),
        out_specs=P(("members", "band", "head"), None),
        check_vma=False,
    )
```

profile of v0, /device:TPU:0, one launch (start us, length us, event | category | flops | bytes accessed | tf_op | source)
XLA Modules:
  0.0 741.7 jit_solution(13681533981195559671)
XLA Ops:
  9.9 22.7 %all_gather.26 = bf16[256,1024]{1,0:T(8,128)(2,1)} all-gather(bf16[256,256]{1,0:T(8,128)(2,1)S(1)} %copy-done.19), channel_id=1, replica_groups=mesh['members'=2,'band'=4,'head'=4] {'band'}, dimensions={1}, use_global_device_ids=true | all-gather | bytes 655360 | tf_op jit(solution)/shard_map/all_gather | solution.py:190
  32.6 19.2 %all-gather.8.cloned.1.call-done = bf16[3,1024,256]{2,1,0:T(8,128)(2,1)} async-done(((bf16[3,256,256]{2,1,0:T(8,128)(2,1)}), bf16[3,1024,256]{2,1,0:T(8,128)(2,1)}) %all-gather.8.cloned.1.call-update) | async-done | bytes 1572880 | tf_op jit(solution)/shard_map/all_gather | solution.py:178
  54.9 3.3 collective-permute-start
  59.8 2.3 convolution_convert_fusion.19
  62.0 7.4 collective-permute-done
  69.4 4.1 collective-permute-done.1
  74.6 59.4 %while.34 = (s32[]{:T(128)}, f32[4,128,256]{2,1,0:T(8,128)}, f32[4,128,4]{1,2,0:T(4,128)S(1)}, s32[4]{0:T(128)S(1)}, s32[4,8]{1,0:T(4,128)S(1)}, /*index=5*/s32[...) while((s32[]{:T(128)}, f32[4,128,256]{2,1,0:T(8,128)}, ...), condition=%wide.region_13.14_spmd, body=%wide.region_4.13_spmd.sunk | while | flops 474056288 | bytes 11562037 | solution.py:137
  137.8 34.9 %all-reduce.5.cloned.1.call-done = bf16[512,1024]{1,0:T(8,128)(2,1)} async-done(((bf16[512,1024]{1,0:T(8,128)(2,1)}), bf16[512,1024]{1,0:T(8,128)(2,1)}) %all-reduce.5.cloned.1.call-update) | async-done | bytes 1048592 | tf_op jit(solution)/shard_map/psum | solution.py:191
  175.3 36.5 %all-gather.10.cloned.1.call-done = bf16[3,1024,256]{2,1,0:T(8,128)(2,1)} async-done(((bf16[3,256,256]{2,1,0:T(8,128)(2,1)}), bf16[3,1024,256]{2,1,0:T(8,128)(2,1)}) %all-gather.10.cloned.1.call-update) | async-done | bytes 1572880 | tf_op jit(solution)/shard_map/all_gather | solution.py:198
  214.9 3.2 collective-permute-start.2
  219.4 47.1 %all_gather.28 = bf16[256,1024]{1,0:T(8,128)(2,1)} all-gather(bf16[256,256]{1,0:T(8,128)(2,1)S(1)} %copy-done.20), channel_id=1, replica_groups=mesh['members'=2,'band'=4,'head'=4] {'band'}, dimensions={1}, use_global_device_ids=true | all-gather | bytes 655360 | tf_op jit(solution)/shard_map/all_gather | solution.py:232
  271.3 2.2 convolution_convert_fusion.16
  275.1 2.8 collective-permute-done.4
  279.0 4.5 collective-permute-done.5
  283.5 33.7 %collective-permute-done.6 = bf16[2,512,256]{2,1,0:T(8,128)(2,1)S(1)} collective-permute-done((bf16[2,512,256]{2,1,0:T(8,128)(2,1)S(1)}, bf16[2,512,256]{2,1,0:T(8,128)(2,1)S(1)}, u32[]{:S(2)}, u32[]{:S(2)}) %collective-permute-start.6) | collective-permute-done | bytes 524320 | tf_op jit(solution)/shard_map/ppermute | solution.py:29
  319.1 92.2 %while.35 = (s32[]{:T(128)}, bf16[4,128,256]{2,1,0:T(8,128)(2,1)S(1)}, s32[4]{0:T(128)S(1)}, s32[]{:T(128)}, s32[2048]{0:T(1024)S(1)}, /*index=5*/s32[]{:T(128)}...) while((s32[]{:T(128)}, ...), condition=%wide.region_27.28_spmd, body=%wide.region_17.27_spmd.sunk | while | flops 422220800 | bytes 58421236 | solution.py:229
  322.9 2.3 fusion.294
  326.1 2.4 fusion.297
  328.5 2.5 fusion.298
  330.9 2.3 fusion.296
  334.7 3.4 fusion.299
  346.0 2.3 fusion.294
  349.2 2.4 fusion.297
  351.5 2.5 fusion.298
  354.0 2.3 fusion.296
  357.8 3.4 fusion.299
  369.0 2.3 fusion.294
  372.2 2.4 fusion.297
  374.6 2.5 fusion.298
  377.1 2.3 fusion.296
  380.9 3.4 fusion.299
  392.1 2.3 fusion.294
  395.3 2.4 fusion.297
  397.6 2.5 fusion.298
  400.1 2.3 fusion.296
  403.9 3.4 fusion.299
  411.3 2.6 convolution_convert_fusion.10
  415.3 33.3 %all-reduce.7.cloned.1.call-done = bf16[512,1024]{1,0:T(8,128)(2,1)} async-done(((bf16[512,1024]{1,0:T(8,128)(2,1)}), bf16[512,1024]{1,0:T(8,128)(2,1)}) %all-reduce.7.cloned.1.call-update) | async-done | bytes 1048592 | tf_op jit(solution)/shard_map/psum | solution.py:233
  451.1 45.2 %all-gather.12.cloned.1.call-done = bf16[1024,1024]{1,0:T(8,128)(2,1)} async-done(((bf16[256,1024]{1,0:T(8,128)(2,1)}), bf16[1024,1024]{1,0:T(8,128)(2,1)}) %all-gather.12.cloned.1.call-update) | async-done | bytes 2097168 | tf_op jit(solution)/shard_map/all_gather | solution.py:238
  496.3 46.5 %all-gather.14.cloned.1.call-done = bf16[1024,1024]{1,0:T(8,128)(2,1)} async-done(((bf16[1024,256]{1,0:T(8,128)(2,1)}), bf16[1024,1024]{1,0:T(8,128)(2,1)}) %all-gather.14.cloned.1.call-update) | async-done | bytes 2097168 | tf_op jit(solution)/shard_map/all_gather | solution.py:241
  542.8 9.5 %convolution_convert_fusion.9 = bf16[512,1024]{1,0:T(8,128)(2,1)} fusion(bf16[1024,1024]{1,0:T(8,128)(2,1)} %all-gather.14.cloned.1.call-done, bf16[1024,1024]{1,0:T(8,128)(2,1)} %all-gather.12.cloned.1.call-done, f32[512,1024]{1,0:T(8,128)S(1)} %get-tuple-element.283, f32[512]{0:T(512)S(1)} %add_rsqrt_fusion.1, f32[512]{0:T(512)S(1)} %broadcast_multiply_fusion.1), kind=kOutput, calls=%fused_computation.216 | convolution fusion | flops 2183659520 | bytes 7344128 | tf_op jit(solution)/shard_map/dot_general | solution.py:63
  553.2 33.8 %all-reduce.9.cloned.1.call-done = bf16[512,1024]{1,0:T(8,128)(2,1)} async-done(((bf16[512,1024]{1,0:T(8,128)(2,1)}), bf16[512,1024]{1,0:T(8,128)(2,1)}) %all-reduce.9.cloned.1.call-update) | async-done | bytes 1048592 | tf_op jit(solution)/shard_map/psum | solution.py:242
  589.5 36.6 %all-gather.6.cloned.1.call-done = bf16[3,1024,256]{2,1,0:T(8,128)(2,1)} async-done(((bf16[3,256,256]{2,1,0:T(8,128)(2,1)}), bf16[3,1024,256]{2,1,0:T(8,128)(2,1)}) %all-gather.6.cloned.1.call-update) | async-done | bytes 1572880 | tf_op jit(solution)/shard_map/all_gather | solution.py:247
  629.3 2.5 collective-permute-start.8
  634.5 25.3 %all_gather.31 = bf16[256,1024]{1,0:T(8,128)(2,1)} all-gather(bf16[256,256]{1,0:T(8,128)(2,1)S(1)} %copy-done.21), channel_id=1, replica_groups=mesh['members'=2,'band'=4,'head'=4] {'band'}, dimensions={1}, use_global_device_ids=true | all-gather | bytes 655360 | tf_op jit(solution)/shard_map/all_gather | solution.py:266
  662.3 45.1 %while.36 = (s32[]{:T(128)}, bf16[4,128,256]{2,1,0:T(8,128)(2,1)}, s32[4]{0:T(128)S(1)}, s32[4,8]{1,0:T(4,128)S(1)}, s32[]{:T(128)}, /*index=5*/s32[4]{0:T(128)}...) while((s32[]{:T(128)}, bf16[4,128,256]{2,1,0:T(8,128)(2,1)}, ...), condition=%wide.region_43.44_spmd, body=%wide.region_34.43_spmd.sunk | while | flops 139755616 | bytes 19489944 | solution.py:137
  707.4 2.6 convolution_convert_fusion.8
  710.0 23.3 %reduce-scatter.2.cloned.1.call-done = bf16[128,1024]{1,0:T(8,128)(2,1)} async-done(((bf16[512,1024]{1,0:T(8,128)(2,1)}), bf16[128,1024]{1,0:T(8,128)(2,1)}) %reduce-scatter.2.cloned.1.call-update) | async-done | bytes 262160 | tf_op jit(solution)/shard_map/reduce_scatter | solution.py:268
  (402 shorter events, 165.6 us)
Async XLA Ops:
  6.5 53.0 %copy-start = (s32[16,8]{0,1:T(8,128)S(1)}, s32[16,8]{0,1:T(8,128)}, u32[]{:S(2)}) copy-start(s32[16,8]{0,1:T(8,128)} %param.31) | copy-start | bytes 1540
  6.5 2.3 copy-start.6
  6.5 2.5 copy-start.13
  6.5 45.2 %all-gather.8.cloned.1.call-start = ((), (), s32[]{:S(2)}) async-start(), calls=%async_computation.2 | async-start | bytes 1966080 | tf_op jit(solution)/shard_map/all_gather | solution.py:178
  7.3 165.4 %all-reduce.5.cloned.1.call-start = ((), (), s32[]{:S(2)}) async-start(), calls=%async_computation.3 | async-start | bytes 2097152 | tf_op jit(solution)/shard_map/psum | solution.py:191
  7.3 2.6 copy-start.19
  53.3 6.4 copy-start.23
  54.9 14.5 %collective-permute-start = (bf16[2,512,256]{2,1,0:T(8,128)(2,1)S(1)}, bf16[2,512,256]{2,1,0:T(8,128)(2,1)S(1)}, u32[]{:S(2)}, u32[]{:S(2)}) collective-permute-start(bf16[2,512,256]{2,1,0:T(8,128)(2,1)S(1)} %pad_maximum_fusion.4), channel_id=1, source_target_pairs={{0,4},{4,8},{8,12},{1,5},{5,9},{9,13},{2,6},{6,10},{10,14},{3,7},{... | collective-permute-start | bytes 1572872 | tf_op jit(solution)/shard_map/ppermute | solution.py:18
  58.2 15.3 %collective-permute-start.1 = (bf16[2,512,256]{2,1,0:T(8,128)(2,1)S(1)}, bf16[2,512,256]{2,1,0:T(8,128)(2,1)S(1)}, u32[]{:S(2)}, u32[]{:S(2)}) collective-permute-start(bf16[2,512,256]{2,1,0:T(8,128)(2,1)S(1)} %pad_maximum_fusion.4), channel_id=1, source_target_pairs={{4,0},{8,4},{12,8},{5,1},{9,5},{13,9},{6,2},{10,6},{14,10},{7,3},{... | collective-permute-start | bytes 1572872 | tf_op jit(solution)/shard_map/ppermute | solution.py:21
  134.0 1.5 copy-start.15
  134.3 38.4 %copy-start.7 = (bf16[512,1024]{1,0:T(8,128)(2,1)S(1)}, bf16[512,1024]{1,0:T(8,128)(2,1)}, u32[]{:S(2)}) copy-start(bf16[512,1024]{1,0:T(8,128)(2,1)} %param.22) | copy-start | bytes 3145732
  137.0 74.8 %all-gather.10.cloned.1.call-start = ((), (), s32[]{:S(2)}) async-start(), calls=%async_computation.4 | async-start | bytes 1966080 | tf_op jit(solution)/shard_map/all_gather | solution.py:198
  137.7 311.0 %all-reduce.7.cloned.1.call-start = ((), (), s32[]{:S(2)}) async-start(), calls=%async_computation.5 | async-start | bytes 2097152 | tf_op jit(solution)/shard_map/psum | solution.py:233
  172.7 1.7 copy-start.9
  213.3 6.2 copy-start.20
  213.3 55.4 %copy-start.18 = (s32[2048]{0:T(1024)S(1)}, s32[2048]{0:T(1024)}, u32[]{:S(2)}) copy-start(s32[2048]{0:T(1024)} %param.35) | copy-start | bytes 24580
  214.9 58.6 %collective-permute-start.2 = (bf16[2,512,256]{2,1,0:T(8,128)(2,1)S(1)}, bf16[2,512,256]{2,1,0:T(8,128)(2,1)S(1)}, u32[]{:S(2)}, u32[]{:S(2)}) collective-permute-start(bf16[2,512,256]{2,1,0:T(8,128)(2,1)S(1)} %pad_maximum_fusion.5), channel_id=1, source_target_pairs={{0,12},{1,13},{2,14},{3,15},{16,28},{17,29},{18,30},{19,31}} | collective-permute-start | bytes 1572872 | tf_op jit(solution)/shard_map/ppermute | solution.py:29
  218.1 56.9 %collective-permute-start.3 = (bf16[2,512,256]{2,1,0:T(8,128)(2,1)S(1)}, bf16[2,512,256]{2,1,0:T(8,128)(2,1)S(1)}, u32[]{:S(2)}, u32[]{:S(2)}) collective-permute-start(bf16[2,512,256]{2,1,0:T(8,128)(2,1)S(1)} %pad_maximum_fusion.5), channel_id=1, source_target_pairs={{0,8},{4,12},{1,9},{5,13},{2,10},{6,14},{3,11},{7,15},{16,24},{20,... | collective-permute-start | bytes 1572872 | tf_op jit(solution)/shard_map/ppermute | solution.py:29
  266.5 11.3 %collective-permute-start.4 = (bf16[2,512,256]{2,1,0:T(8,128)(2,1)S(1)}, bf16[2,512,256]{2,1,0:T(8,128)(2,1)}, u32[]{:S(2)}, u32[]{:S(2)}) collective-permute-start(bf16[2,512,256]{2,1,0:T(8,128)(2,1)S(1)} %pad_maximum_fusion.5), channel_id=1, source_target_pairs={{0,4},{4,8},{8,12},{1,5},{5,9},{9,13},{2,6},{6,10},{10,14},{3,7},{... | collective-permute-start | bytes 1572872 | tf_op jit(solution)/shard_map/ppermute | solution.py:29
  268.7 14.7 %collective-permute-start.5 = (bf16[2,512,256]{2,1,0:T(8,128)(2,1)S(1)}, bf16[2,512,256]{2,1,0:T(8,128)(2,1)S(1)}, u32[]{:S(2)}, u32[]{:S(2)}) collective-permute-start(bf16[2,512,256]{2,1,0:T(8,128)(2,1)S(1)} %pad_maximum_fusion.5), channel_id=1, source_target_pairs={{4,0},{8,4},{12,8},{5,1},{9,5},{13,9},{6,2},{10,6},{14,10},{7,3},{... | collective-permute-start | bytes 1572872 | tf_op jit(solution)/shard_map/ppermute | solution.py:29
  270.0 47.2 %collective-permute-start.6 = (bf16[2,512,256]{2,1,0:T(8,128)(2,1)S(1)}, bf16[2,512,256]{2,1,0:T(8,128)(2,1)S(1)}, u32[]{:S(2)}, u32[]{:S(2)}) collective-permute-start(bf16[2,512,256]{2,1,0:T(8,128)(2,1)S(1)} %pad_maximum_fusion.5), channel_id=1, source_target_pairs={{8,0},{12,4},{9,1},{13,5},{10,2},{14,6},{11,3},{15,7},{24,16},{28,... | collective-permute-start | bytes 1572872 | tf_op jit(solution)/shard_map/ppermute | solution.py:29
  273.5 43.7 %collective-permute-start.7 = (bf16[2,512,256]{2,1,0:T(8,128)(2,1)S(1)}, bf16[2,512,256]{2,1,0:T(8,128)(2,1)S(1)}, u32[]{:S(2)}, u32[]{:S(2)}) collective-permute-start(bf16[2,512,256]{2,1,0:T(8,128)(2,1)S(1)} %pad_maximum_fusion.5), channel_id=1, source_target_pairs={{12,0},{13,1},{14,2},{15,3},{28,16},{29,17},{30,18},{31,19}} | collective-permute-start | bytes 1572872 | tf_op jit(solution)/shard_map/ppermute | solution.py:29
  317.3 1.8 copy-start.2
  334.7 3.4 copy-start.5
  357.8 3.4 copy-start.5
  380.8 3.4 copy-start.5
  403.9 3.4 copy-start.5
  411.3 37.4 %copy-start.8 = (bf16[512,1024]{1,0:T(8,128)(2,1)S(1)}, bf16[512,1024]{1,0:T(8,128)(2,1)}, u32[]{:S(2)}) copy-start(bf16[512,1024]{1,0:T(8,128)(2,1)} %param.22) | copy-start | bytes 3145732
  413.9 82.4 %all-gather.12.cloned.1.call-start = ((), (), s32[]{:S(2)}) async-start(), calls=%async_computation.6 | async-start | bytes 2621440 | tf_op jit(solution)/shard_map/all_gather | solution.py:238
  414.5 128.3 %all-gather.14.cloned.1.call-start = ((), (), s32[]{:S(2)}) async-start(), calls=%async_computation.7 | async-start | bytes 2621440 | tf_op jit(solution)/shard_map/all_gather | solution.py:241
  415.1 171.9 %all-reduce.9.cloned.1.call-start = ((), (), s32[]{:S(2)}) async-start(), calls=%async_computation.8 | async-start | bytes 2097152 | tf_op jit(solution)/shard_map/psum | solution.py:242
  552.4 73.7 %all-gather.6.cloned.1.call-start = ((), (), s32[]{:S(2)}) async-start(), calls=%async_computation.1 | async-start | bytes 1966080 | tf_op jit(solution)/shard_map/all_gather | solution.py:247
  553.1 180.3 %reduce-scatter.2.cloned.1.call-start = ((), (), s32[]{:S(2)}) async-start(), calls=%async_computation.9 | async-start | bytes 1310720 | tf_op jit(solution)/shard_map/reduce_scatter | solution.py:268
  587.0 1.6 copy-start.12
  627.6 5.5 copy-start.22
  627.6 6.9 copy-start.21
  627.6 32.2 %copy-start.14 = (bf16[512,1024]{1,0:T(8,128)(2,1)S(1)}, bf16[512,1024]{1,0:T(8,128)(2,1)}, u32[]{:S(2)}) copy-start(bf16[512,1024]{1,0:T(8,128)(2,1)} %param.21) | copy-start | bytes 3145732
  629.3 32.1 %collective-permute-start.8 = (bf16[2,512,256]{2,1,0:T(8,128)(2,1)S(1)}, bf16[2,512,256]{2,1,0:T(8,128)(2,1)S(1)}, u32[]{:S(2)}, u32[]{:S(2)}) collective-permute-start(bf16[2,512,256]{2,1,0:T(8,128)(2,1)S(1)} %pad_maximum_fusion.6), channel_id=1, source_target_pairs={{0,4},{4,8},{8,12},{1,5},{5,9},{9,13},{2,6},{6,10},{10,14},{3,7},{... | collective-permute-start | bytes 1572872 | tf_op jit(solution)/shard_map/ppermute | solution.py:18
  631.8 29.5 %collective-permute-start.9 = (bf16[2,512,256]{2,1,0:T(8,128)(2,1)S(1)}, bf16[2,512,256]{2,1,0:T(8,128)(2,1)S(1)}, u32[]{:S(2)}, u32[]{:S(2)}) collective-permute-start(bf16[2,512,256]{2,1,0:T(8,128)(2,1)S(1)} %pad_maximum_fusion.6), channel_id=1, source_target_pairs={{4,0},{8,4},{12,8},{5,1},{9,5},{13,9},{6,2},{10,6},{14,10},{7,3},{... | collective-permute-start | bytes 1572872 | tf_op jit(solution)/shard_map/ppermute | solution.py:21
  662.3 6.0 copy-start.10
  662.3 6.8 copy-start.16
  673.6 6.1 copy-start.10
  673.6 6.8 copy-start.16
  684.9 6.1 copy-start.10
  684.9 6.8 copy-start.16
  696.1 6.1 copy-start.10
  696.1 6.8 copy-start.16
  707.4 27.7 %copy-start.1 = (s32[16,8]{0,1:T(8,128)S(1)}, s32[16,8]{0,1:T(8,128)}, u32[]{:S(2)}) copy-start(s32[16,8]{0,1:T(8,128)} %param.31) | copy-start | bytes 1540
  (16 other events, 21.2 us)
Sparse Core Ops, SparseCore 0:
  8.9 42.8 all-gather.7
  137.1 35.5 all-reduce.4
  174.2 37.4 all-gather.9
  414.0 34.6 all-reduce.6
  450.1 46.1 all-gather.11
  497.7 45.0 all-gather.13
  552.5 34.4 all-reduce.8
  588.6 37.4 all-gather.5
  710.1 23.1 reduce-scatter.1
where the time goes:
time: 746 us; the launch traced here: 742 us
  waiting for transfers between devices  365 us (49%)
  matrix products  120 us (16%)
  blocking collectives  95 us (13%)
  local copies, waits for them, and re-layouts  60.9 us (8%)
  other arithmetic  41.2 us (6%)
  loops' own time  26.4 us (4%)
  starting transfers between devices  19.6 us (3%)
  between operations  13.7 us (2%)
    dot_general x48, matrix products, head_scores(): jnp.einsum('qd,kd->qk', queries[:, lower:lower + HD], key_rows[:, lower:l...  61.3 us
    all_gather x1, blocking collectives, per_device(): lax.all_gather(proc_out, 'band', axis=1, tiled=True)  47.1 us
    all_gather x1, waiting for transfers between devices, per_device(): lax.all_gather(ff_down, 'band', axis=1, tiled=True)  46.5 us
    all_gather x1, waiting for transfers between devices, per_device(): lax.all_gather(ff_up, 'band', axis=0, tiled=True)  45.2 us
    ppermute x6, waiting for transfers between devices, shifted(): return lax.ppermute(block, axis, route)  41 us
    all_gather x1, waiting for transfers between devices, per_device(): lax.all_gather(dec_in, 'band', axis=1, tiled=True)  36.6 us
    all_gather x1, waiting for transfers between devices, per_device(): lax.all_gather(proc_in, 'band', axis=1, tiled=True)  36.5 us
    psum x1, waiting for transfers between devices, per_device(): lax.psum(enc_terms.astype(jnp.bfloat16), 'head').astype(jnp.float32)  34.9 us
  transfers between devices with their start and end apart: 19, of which 14 were waited for; matrix products, arithmetic and copies ran while one was open for 3% of the time, Pallas kernels for 0%

commit v1 on v0

--- a/solution.py
+++ b/solution.py
@@ -8,6 +8,18 @@
 WINDOW = 1536
 EPSILON = 1e-05
 NEGATIVE = -1e30
+
+
+def ring_gather(array, axis, dim):
+    ways, here, turn = (lax.axis_size(axis), lax.axis_index(axis), array.shape[dim])
+    lengths = [n * ways if d == dim else n for d, n in enumerate(array.shape)]
+    full = lax.dynamic_update_slice_in_dim(
+        jnp.zeros(lengths, array.dtype), array, here * turn, axis=dim
+    )
+    for far in range(1, ways):
+        array = lax.ppermute(array, axis, [(d, (d + 1) % ways) for d in range(ways)])
+        full = lax.dynamic_update_slice_in_dim(full, array, (here - far) % ways * turn, axis=dim)
+    return full
 
 
 def padded(block, sides, width):
@@ -229,7 +241,7 @@
     proc_attn = lax.map(window_block, jnp.arange(mesh_blocks, dtype=jnp.int32)).reshape(
         mesh_rows, width
     )
-    proc_terms = columns_of(proc_attn, lax.all_gather(proc_out, "band", axis=1, tiled=True))
+    proc_terms = columns_of(proc_attn, ring_gather(proc_out, "band", 1))
     mesh_mid = mesh_state + lax.psum(proc_terms.astype(jnp.bfloat16), "head").astype(jnp.float32)
     ff_norm = normed(mesh_mid)
     hidden = fold_rows(

time: 746 us -> 698 us (0.936)
  blocking collectives: 95 us -> 47.9 us
    all_gather x1 -> x0, blocking collectives: 47.1 us -> none  [per_device(): lax.all_gather(proc_out, 'band', axis=1, tiled=True)]
    psum x1, waiting for transfers between devices: 34.9 us -> 21.3 us  [per_device(): lax.psum(enc_terms.astype(jnp.bfloat16), 'head').astype(jnp.float32)]
    ppermute x0 -> x3, waiting for transfers between devices: none -> 11.8 us  [ring_gather(): lax.ppermute(array, axis, [(d, (d + 1) % ways) for d in range(ways)])]
  transfers between devices with their start and end apart: 19 -> 22, of which waited for: 14 -> 17; matrix products, arithmetic and copies ran while one was open for 3% -> 3% of each run, Pallas kernels for 0% -> 0%
where the time goes in v1:
time: 698 us; the launch traced here: 694 us
  waiting for transfers between devices  365 us (52%)
  matrix products  118 us (17%)
  local copies, waits for them, and re-layouts  60 us (9%)
  blocking collectives  47.9 us (7%)
  other arithmetic  41.2 us (6%)
  loops' own time  26.4 us (4%)
  starting transfers between devices  21.6 us (3%)
  between operations  13.8 us (2%)
    dot_general x48, matrix products, head_scores(): jnp.einsum('qd,kd->qk', queries[:, lower:lower + HD], key_rows[:, lower:l...  61.3 us
    all_gather x1, waiting for transfers between devices, per_device(): lax.all_gather(ff_down, 'band', axis=1, tiled=True)  46.5 us
    all_gather x1, waiting for transfers between devices, per_device(): lax.all_gather(ff_up, 'band', axis=0, tiled=True)  45.2 us
    ppermute x6, waiting for transfers between devices, shifted(): return lax.ppermute(block, axis, route)  42.9 us
    all_gather x1, waiting for transfers between devices, per_device(): lax.all_gather(dec_in, 'band', axis=1, tiled=True)  36.6 us
    all_gather x1, waiting for transfers between devices, per_device(): lax.all_gather(proc_in, 'band', axis=1, tiled=True)  36.5 us
    psum x1, waiting for transfers between devices, per_device(): lax.psum(ff_terms.astype(jnp.bfloat16), 'head').astype(jnp.float32)  33.8 us
    psum x1, waiting for transfers between devices, per_device(): lax.psum(proc_terms.astype(jnp.bfloat16), 'head').astype(jnp.float32)  33.4 us
  transfers between devices with their start and end apart: 22, of which 17 were waited for; matrix products, arithmetic and copies ran while one was open for 3% of the time, Pallas kernels for 0%

profile of v1, /device:TPU:0, one launch (start us, length us, event | category | flops | bytes accessed | tf_op | source)
XLA Modules:
  0.0 693.8 jit_solution(273857339639091701)
XLA Ops:
  9.9 22.7 %all_gather.23 = bf16[256,1024]{1,0:T(8,128)(2,1)} all-gather(bf16[256,256]{1,0:T(8,128)(2,1)S(1)} %copy-done.20), channel_id=1, replica_groups=mesh['members'=2,'band'=4,'head'=4] {'band'}, dimensions={1}, use_global_device_ids=true | all-gather | bytes 655360 | tf_op jit(solution)/shard_map/all_gather | solution.py:202
  32.6 19.2 %all-gather.8.cloned.1.call-done = bf16[3,1024,256]{2,1,0:T(8,128)(2,1)} async-done(((bf16[3,256,256]{2,1,0:T(8,128)(2,1)}), bf16[3,1024,256]{2,1,0:T(8,128)(2,1)}) %all-gather.8.cloned.1.call-update) | async-done | bytes 1572880 | tf_op jit(solution)/shard_map/all_gather | solution.py:190
  54.9 3.3 collective-permute-start
  62.0 7.4 %collective-permute-done = bf16[2,512,256]{2,1,0:T(8,128)(2,1)S(1)} collective-permute-done((bf16[2,512,256]{2,1,0:T(8,128)(2,1)S(1)}, bf16[2,512,256]{2,1,0:T(8,128)(2,1)S(1)}, u32[]{:S(2)}, u32[]{:S(2)}) %collective-permute-start) | collective-permute-done | bytes 524320 | tf_op jit(solution)/shard_map/ppermute | solution.py:30
  69.4 4.1 collective-permute-done.1
  74.6 59.4 %while.34 = (s32[]{:T(128)}, f32[4,128,256]{2,1,0:T(8,128)}, f32[4,128,4]{1,2,0:T(4,128)S(1)}, s32[4]{0:T(128)S(1)}, s32[4,8]{1,0:T(4,128)S(1)}, /*index=5*/s32[...) while((s32[]{:T(128)}, f32[4,128,256]{2,1,0:T(8,128)}, ...), condition=%wide.region_13.14_spmd, body=%wide.region_4.13_spmd.sunk | while | flops 474056288 | bytes 11562037 | solution.py:149
  139.4 5.2 collective-permute-done.8
  144.8 6.6 collective-permute-done.9
  151.3 21.3 %all-reduce.5.cloned.1.call-done = bf16[512,1024]{1,0:T(8,128)(2,1)} async-done(((bf16[512,1024]{1,0:T(8,128)(2,1)}), bf16[512,1024]{1,0:T(8,128)(2,1)}) %all-reduce.5.cloned.1.call-update) | async-done | bytes 1048592 | tf_op jit(solution)/shard_map/psum | solution.py:203
  175.3 36.5 %all-gather.10.cloned.1.call-done = bf16[3,1024,256]{2,1,0:T(8,128)(2,1)} async-done(((bf16[3,256,256]{2,1,0:T(8,128)(2,1)}), bf16[3,1024,256]{2,1,0:T(8,128)(2,1)}) %all-gather.10.cloned.1.call-update) | async-done | bytes 1572880 | tf_op jit(solution)/shard_map/all_gather | solution.py:210
  213.9 3.2 collective-permute-start.2
  218.5 2.5 collective-permute-start.4
  224.7 4.7 collective-permute-done.2
  231.0 9.7 %collective-permute-done.3 = bf16[2,512,256]{2,1,0:T(8,128)(2,1)S(1)} collective-permute-done((bf16[2,512,256]{2,1,0:T(8,128)(2,1)S(1)}, bf16[2,512,256]{2,1,0:T(8,128)(2,1)S(1)}, u32[]{:S(2)}, u32[]{:S(2)}) %collective-permute-start.3) | collective-permute-done | bytes 524320 | tf_op jit(solution)/shard_map/ppermute | solution.py:41
  240.7 10.0 %collective-permute-done.4 = bf16[2,512,256]{2,1,0:T(8,128)(2,1)S(1)} collective-permute-done((bf16[2,512,256]{2,1,0:T(8,128)(2,1)S(1)}, bf16[2,512,256]{2,1,0:T(8,128)(2,1)S(1)}, u32[]{:S(2)}, u32[]{:S(2)}) %collective-permute-start.4) | collective-permute-done | bytes 524320 | tf_op jit(solution)/shard_map/ppermute | solution.py:41
  250.8 18.5 %collective-permute-done.6 = bf16[2,512,256]{2,1,0:T(8,128)(2,1)S(1)} collective-permute-done((bf16[2,512,256]{2,1,0:T(8,128)(2,1)S(1)}, bf16[2,512,256]{2,1,0:T(8,128)(2,1)S(1)}, u32[]{:S(2)}, u32[]{:S(2)}) %collective-permute-start.6) | collective-permute-done | bytes 524320 | tf_op jit(solution)/shard_map/ppermute | solution.py:41
  271.2 92.2 %while.35 = (s32[]{:T(128)}, bf16[4,128,256]{2,1,0:T(8,128)(2,1)S(1)}, s32[4]{0:T(128)S(1)}, s32[]{:T(128)}, s32[2048]{0:T(1024)S(1)}, /*index=5*/s32[]{:T(128)}...) while((s32[]{:T(128)}, ...), condition=%wide.region_27.28_spmd, body=%wide.region_17.27_spmd.sunk | while | flops 422220800 | bytes 58421236 | solution.py:241
  275.0 2.3 fusion.294
  278.2 2.4 fusion.297
  280.6 2.5 fusion.298
  283.1 2.3 fusion.296
  286.8 3.4 fusion.299
  298.1 2.3 fusion.294
  301.3 2.4 fusion.297
  303.6 2.5 fusion.298
  306.1 2.3 fusion.296
  309.9 3.4 fusion.299
  321.2 2.3 fusion.294
  324.3 2.4 fusion.297
  326.7 2.5 fusion.298
  329.2 2.3 fusion.296
  333.0 3.4 fusion.299
  347.4 2.4 fusion.297
  349.8 2.5 fusion.298
  352.2 2.3 fusion.296
  356.0 3.4 fusion.299
  363.4 2.6 convolution_convert_fusion.10
  367.5 33.4 %all-reduce.7.cloned.1.call-done = bf16[512,1024]{1,0:T(8,128)(2,1)} async-done(((bf16[512,1024]{1,0:T(8,128)(2,1)}), bf16[512,1024]{1,0:T(8,128)(2,1)}) %all-reduce.7.cloned.1.call-update) | async-done | bytes 1048592 | tf_op jit(solution)/shard_map/psum | solution.py:245
  403.2 45.2 %all-gather.12.cloned.1.call-done = bf16[1024,1024]{1,0:T(8,128)(2,1)} async-done(((bf16[256,1024]{1,0:T(8,128)(2,1)}), bf16[1024,1024]{1,0:T(8,128)(2,1)}) %all-gather.12.cloned.1.call-update) | async-done | bytes 2097168 | tf_op jit(solution)/shard_map/all_gather | solution.py:250
  448.4 46.5 %all-gather.14.cloned.1.call-done = bf16[1024,1024]{1,0:T(8,128)(2,1)} async-done(((bf16[1024,256]{1,0:T(8,128)(2,1)}), bf16[1024,1024]{1,0:T(8,128)(2,1)}) %all-gather.14.cloned.1.call-update) | async-done | bytes 2097168 | tf_op jit(solution)/shard_map/all_gather | solution.py:253
  494.9 9.6 %convolution_convert_fusion.9 = bf16[512,1024]{1,0:T(8,128)(2,1)} fusion(bf16[1024,1024]{1,0:T(8,128)(2,1)} %all-gather.14.cloned.1.call-done, bf16[1024,1024]{1,0:T(8,128)(2,1)} %all-gather.12.cloned.1.call-done, f32[512,1024]{1,0:T(8,128)S(1)} %get-tuple-element.283, f32[512]{0:T(512)S(1)} %add_rsqrt_fusion.1, f32[512]{0:T(512)S(1)} %broadcast_multiply_fusion.1), kind=kOutput, calls=%fused_computation.216 | convolution fusion | flops 2183659520 | bytes 7344128 | tf_op jit(solution)/shard_map/dot_general | solution.py:75
  505.3 33.8 %all-reduce.9.cloned.1.call-done = bf16[512,1024]{1,0:T(8,128)(2,1)} async-done(((bf16[512,1024]{1,0:T(8,128)(2,1)}), bf16[512,1024]{1,0:T(8,128)(2,1)}) %all-reduce.9.cloned.1.call-update) | async-done | bytes 1048592 | tf_op jit(solution)/shard_map/psum | solution.py:254
  541.6 36.6 %all-gather.6.cloned.1.call-done = bf16[3,1024,256]{2,1,0:T(8,128)(2,1)} async-done(((bf16[3,256,256]{2,1,0:T(8,128)(2,1)}), bf16[3,1024,256]{2,1,0:T(8,128)(2,1)}) %all-gather.6.cloned.1.call-update) | async-done | bytes 1572880 | tf_op jit(solution)/shard_map/all_gather | solution.py:259
  581.4 2.5 collective-permute-start.11
  586.6 25.3 %all_gather.27 = bf16[256,1024]{1,0:T(8,128)(2,1)} all-gather(bf16[256,256]{1,0:T(8,128)(2,1)S(1)} %copy-done.21), channel_id=1, replica_groups=mesh['members'=2,'band'=4,'head'=4] {'band'}, dimensions={1}, use_global_device_ids=true | all-gather | bytes 655360 | tf_op jit(solution)/shard_map/all_gather | solution.py:278
  614.4 45.1 %while.36 = (s32[]{:T(128)}, bf16[4,128,256]{2,1,0:T(8,128)(2,1)}, s32[4]{0:T(128)S(1)}, s32[4,8]{1,0:T(4,128)S(1)}, s32[]{:T(128)}, /*index=5*/s32[4]{0:T(128)}...) while((s32[]{:T(128)}, bf16[4,128,256]{2,1,0:T(8,128)(2,1)}, ...), condition=%wide.region_43.44_spmd, body=%wide.region_34.43_spmd.sunk | while | flops 139755616 | bytes 19489944 | solution.py:149
  659.5 2.6 convolution_convert_fusion.8
  662.1 23.4 %reduce-scatter.2.cloned.1.call-done = bf16[128,1024]{1,0:T(8,128)(2,1)} async-done(((bf16[512,1024]{1,0:T(8,128)(2,1)}), bf16[128,1024]{1,0:T(8,128)(2,1)}) %reduce-scatter.2.cloned.1.call-update) | async-done | bytes 262160 | tf_op jit(solution)/shard_map/reduce_scatter | solution.py:280
  (416 shorter events, 168.9 us)
Async XLA Ops:
  6.5 53.0 %copy-start = (s32[16,8]{0,1:T(8,128)S(1)}, s32[16,8]{0,1:T(8,128)}, u32[]{:S(2)}) copy-start(s32[16,8]{0,1:T(8,128)} %param.31) | copy-start | bytes 1540
  6.5 2.3 copy-start.6
  6.5 2.5 copy-start.13
  6.5 45.2 %all-gather.8.cloned.1.call-start = ((), (), s32[]{:S(2)}) async-start(), calls=%async_computation.2 | async-start | bytes 1966080 | tf_op jit(solution)/shard_map/all_gather | solution.py:190
  7.3 165.4 %all-reduce.5.cloned.1.call-start = ((), (), s32[]{:S(2)}) async-start(), calls=%async_computation.3 | async-start | bytes 2097152 | tf_op jit(solution)/shard_map/psum | solution.py:203
  7.3 2.6 copy-start.20
  53.3 6.4 copy-start.25
  54.9 14.5 %collective-permute-start = (bf16[2,512,256]{2,1,0:T(8,128)(2,1)S(1)}, bf16[2,512,256]{2,1,0:T(8,128)(2,1)S(1)}, u32[]{:S(2)}, u32[]{:S(2)}) collective-permute-start(bf16[2,512,256]{2,1,0:T(8,128)(2,1)S(1)} %pad_maximum_fusion.4), channel_id=1, source_target_pairs={{0,4},{4,8},{8,12},{1,5},{5,9},{9,13},{2,6},{6,10},{10,14},{3,7},{... | collective-permute-start | bytes 1572872 | tf_op jit(solution)/shard_map/ppermute | solution.py:30
  58.2 15.3 %collective-permute-start.1 = (bf16[2,512,256]{2,1,0:T(8,128)(2,1)S(1)}, bf16[2,512,256]{2,1,0:T(8,128)(2,1)S(1)}, u32[]{:S(2)}, u32[]{:S(2)}) collective-permute-start(bf16[2,512,256]{2,1,0:T(8,128)(2,1)S(1)} %pad_maximum_fusion.4), channel_id=1, source_target_pairs={{4,0},{8,4},{12,8},{5,1},{9,5},{13,9},{6,2},{10,6},{14,10},{7,3},{... | collective-permute-start | bytes 1572872 | tf_op jit(solution)/shard_map/ppermute | solution.py:33
  134.3 3.4 copy-start.22
  134.3 10.3 %copy-start.19 = (s32[2048]{0:T(1024)S(1)}, s32[2048]{0:T(1024)}, u32[]{:S(2)}) copy-start(s32[2048]{0:T(1024)} %param.35) | copy-start | bytes 24580
  135.5 37.1 %copy-start.7 = (bf16[512,1024]{1,0:T(8,128)(2,1)S(1)}, bf16[512,1024]{1,0:T(8,128)(2,1)}, u32[]{:S(2)}) copy-start(bf16[512,1024]{1,0:T(8,128)(2,1)} %param.22) | copy-start | bytes 3145732
  137.0 74.8 %all-gather.10.cloned.1.call-start = ((), (), s32[]{:S(2)}) async-start(), calls=%async_computation.4 | async-start | bytes 1966080 | tf_op jit(solution)/shard_map/all_gather | solution.py:210
  137.7 263.1 %all-reduce.7.cloned.1.call-start = ((), (), s32[]{:S(2)}) async-start(), calls=%async_computation.5 | async-start | bytes 2097152 | tf_op jit(solution)/shard_map/psum | solution.py:245
  137.8 6.8 collective-permute-start.8
  144.6 6.8 collective-permute-start.9
  151.3 69.6 %collective-permute-start.10 = (bf16[256,256]{1,0:T(8,128)(2,1)S(1)}, bf16[256,256]{1,0:T(8,128)(2,1)S(1)}, u32[]{:S(2)}, u32[]{:S(2)}) collective-permute-start(bf16[256,256]{1,0:T(8,128)(2,1)S(1)} %collective-permute-done.9), channel_id=1, source_target_pairs={{0,4},{4,8},{8,12},{12,0},{1,5},{5,9},{9,13},{13,1},{2,6},{6,10},{... | collective-permute-start | bytes 393224 | tf_op jit(solution)/shard_map/ppermute | solution.py:20
  213.9 15.6 %collective-permute-start.2 = (bf16[2,512,256]{2,1,0:T(8,128)(2,1)S(1)}, bf16[2,512,256]{2,1,0:T(8,128)(2,1)S(1)}, u32[]{:S(2)}, u32[]{:S(2)}) collective-permute-start(bf16[2,512,256]{2,1,0:T(8,128)(2,1)S(1)} %pad_maximum_fusion.5), channel_id=1, source_target_pairs={{0,12},{1,13},{2,14},{3,15},{16,28},{17,29},{18,30},{19,31}} | collective-permute-start | bytes 1572872 | tf_op jit(solution)/shard_map/ppermute | solution.py:41
  217.1 23.6 %collective-permute-start.3 = (bf16[2,512,256]{2,1,0:T(8,128)(2,1)S(1)}, bf16[2,512,256]{2,1,0:T(8,128)(2,1)S(1)}, u32[]{:S(2)}, u32[]{:S(2)}) collective-permute-start(bf16[2,512,256]{2,1,0:T(8,128)(2,1)S(1)} %pad_maximum_fusion.5), channel_id=1, source_target_pairs={{0,8},{4,12},{1,9},{5,13},{2,10},{6,14},{3,11},{7,15},{16,24},{20,... | collective-permute-start | bytes 1572872 | tf_op jit(solution)/shard_map/ppermute | solution.py:41
  218.5 32.2 %collective-permute-start.4 = (bf16[2,512,256]{2,1,0:T(8,128)(2,1)S(1)}, bf16[2,512,256]{2,1,0:T(8,128)(2,1)S(1)}, u32[]{:S(2)}, u32[]{:S(2)}) collective-permute-start(bf16[2,512,256]{2,1,0:T(8,128)(2,1)S(1)} %pad_maximum_fusion.5), channel_id=1, source_target_pairs={{0,4},{4,8},{8,12},{1,5},{5,9},{9,13},{2,6},{6,10},{10,14},{3,7},{... | collective-permute-start | bytes 1572872 | tf_op jit(solution)/shard_map/ppermute | solution.py:41
  221.0 19.7 %copy-start.16 = (bf16[256,1024]{1,0:T(8,128)(2,1)}, bf16[256,1024]{1,0:T(8,128)(2,1)S(1)}, u32[]{:S(2)}) copy-start(bf16[256,1024]{1,0:T(8,128)(2,1)S(1)} %constant_dynamic-update-slice_fusion.10) | copy-start | bytes 1572868
  221.0 29.8 %collective-permute-start.5 = (bf16[2,512,256]{2,1,0:T(8,128)(2,1)S(1)}, bf16[2,512,256]{2,1,0:T(8,128)(2,1)S(1)}, u32[]{:S(2)}, u32[]{:S(2)}) collective-permute-start(bf16[2,512,256]{2,1,0:T(8,128)(2,1)S(1)} %pad_maximum_fusion.5), channel_id=1, source_target_pairs={{4,0},{8,4},{12,8},{5,1},{9,5},{13,9},{6,2},{10,6},{14,10},{7,3},{... | collective-permute-start | bytes 1572872 | tf_op jit(solution)/shard_map/ppermute | solution.py:41
  222.3 47.0 %collective-permute-start.6 = (bf16[2,512,256]{2,1,0:T(8,128)(2,1)S(1)}, bf16[2,512,256]{2,1,0:T(8,128)(2,1)S(1)}, u32[]{:S(2)}, u32[]{:S(2)}) collective-permute-start(bf16[2,512,256]{2,1,0:T(8,128)(2,1)S(1)} %pad_maximum_fusion.5), channel_id=1, source_target_pairs={{8,0},{12,4},{9,1},{13,5},{10,2},{14,6},{11,3},{15,7},{24,16},{28,... | collective-permute-start | bytes 1572872 | tf_op jit(solution)/shard_map/ppermute | solution.py:41
  229.4 39.9 %collective-permute-start.7 = (bf16[2,512,256]{2,1,0:T(8,128)(2,1)S(1)}, bf16[2,512,256]{2,1,0:T(8,128)(2,1)S(1)}, u32[]{:S(2)}, u32[]{:S(2)}) collective-permute-start(bf16[2,512,256]{2,1,0:T(8,128)(2,1)S(1)} %pad_maximum_fusion.5), channel_id=1, source_target_pairs={{12,0},{13,1},{14,2},{15,3},{28,16},{29,17},{30,18},{31,19}} | collective-permute-start | bytes 1572872 | tf_op jit(solution)/shard_map/ppermute | solution.py:41
  286.8 3.4 copy-start.5
  309.9 3.4 copy-start.5
  333.0 3.4 copy-start.5
  356.0 3.4 copy-start.5
  363.4 37.4 %copy-start.8 = (bf16[512,1024]{1,0:T(8,128)(2,1)S(1)}, bf16[512,1024]{1,0:T(8,128)(2,1)}, u32[]{:S(2)}) copy-start(bf16[512,1024]{1,0:T(8,128)(2,1)} %param.22) | copy-start | bytes 3145732
  366.0 82.4 %all-gather.12.cloned.1.call-start = ((), (), s32[]{:S(2)}) async-start(), calls=%async_computation.6 | async-start | bytes 2621440 | tf_op jit(solution)/shard_map/all_gather | solution.py:250
  366.6 128.3 %all-gather.14.cloned.1.call-start = ((), (), s32[]{:S(2)}) async-start(), calls=%async_computation.7 | async-start | bytes 2621440 | tf_op jit(solution)/shard_map/all_gather | solution.py:253
  367.2 171.9 %all-reduce.9.cloned.1.call-start = ((), (), s32[]{:S(2)}) async-start(), calls=%async_computation.8 | async-start | bytes 2097152 | tf_op jit(solution)/shard_map/psum | solution.py:254
  504.5 73.7 %all-gather.6.cloned.1.call-start = ((), (), s32[]{:S(2)}) async-start(), calls=%async_computation.1 | async-start | bytes 1966080 | tf_op jit(solution)/shard_map/all_gather | solution.py:259
  505.2 180.3 %reduce-scatter.2.cloned.1.call-start = ((), (), s32[]{:S(2)}) async-start(), calls=%async_computation.9 | async-start | bytes 1310720 | tf_op jit(solution)/shard_map/reduce_scatter | solution.py:280
  579.7 5.5 copy-start.23
  579.7 6.9 copy-start.21
  579.7 32.2 %copy-start.14 = (bf16[512,1024]{1,0:T(8,128)(2,1)S(1)}, bf16[512,1024]{1,0:T(8,128)(2,1)}, u32[]{:S(2)}) copy-start(bf16[512,1024]{1,0:T(8,128)(2,1)} %param.21) | copy-start | bytes 3145732
  581.4 32.1 %collective-permute-start.11 = (bf16[2,512,256]{2,1,0:T(8,128)(2,1)S(1)}, bf16[2,512,256]{2,1,0:T(8,128)(2,1)S(1)}, u32[]{:S(2)}, u32[]{:S(2)}) collective-permute-start(bf16[2,512,256]{2,1,0:T(8,128)(2,1)S(1)} %pad_maximum_fusion.6), channel_id=1, source_target_pairs={{0,4},{4,8},{8,12},{1,5},{5,9},{9,13},{2,6},{6,10},{10,14},{3,7},{... | collective-permute-start | bytes 1572872 | tf_op jit(solution)/shard_map/ppermute | solution.py:30
  583.9 29.5 %collective-permute-start.12 = (bf16[2,512,256]{2,1,0:T(8,128)(2,1)S(1)}, bf16[2,512,256]{2,1,0:T(8,128)(2,1)S(1)}, u32[]{:S(2)}, u32[]{:S(2)}) collective-permute-start(bf16[2,512,256]{2,1,0:T(8,128)(2,1)S(1)} %pad_maximum_fusion.6), channel_id=1, source_target_pairs={{4,0},{8,4},{12,8},{5,1},{9,5},{13,9},{6,2},{10,6},{14,10},{7,3},{... | collective-permute-start | bytes 1572872 | tf_op jit(solution)/shard_map/ppermute | solution.py:33
  614.4 6.0 copy-start.10
  614.4 6.8 copy-start.17
  625.7 6.1 copy-start.10
  625.7 6.8 copy-start.17
  637.0 6.1 copy-start.10
  637.0 6.8 copy-start.17
  648.2 6.1 copy-start.10
  648.3 6.8 copy-start.17
  659.5 27.8 %copy-start.1 = (s32[16,8]{0,1:T(8,128)S(1)}, s32[16,8]{0,1:T(8,128)}, u32[]{:S(2)}) copy-start(s32[16,8]{0,1:T(8,128)} %param.31) | copy-start | bytes 1540
  (21 other events, 29.4 us)
Sparse Core Ops, SparseCore 0:
  8.9 42.8 all-gather.7
  137.1 35.5 all-reduce.4
  174.2 37.4 all-gather.9
  366.1 34.6 all-reduce.6
  402.2 46.1 all-gather.11
  449.8 45.0 all-gather.13
  504.6 34.4 all-reduce.8
  540.7 37.4 all-gather.5
  662.2 23.2 reduce-scatter.1
